TPU v7x, 512 devices: a whole 4x8x8 slice. The times are simulated.
512 devices in a mesh: task: 4 (over y_lo), tok: 128 (over z, y_hi, x, core).
Axes of the slice: x: 4, y: 8 (y_hi: 2, y_lo: 4; y = y_hi * 4 + y_lo), z: 8, core: 2. Of those that a mesh axis runs over, the one named last changes fastest.
Arguments:
- hidden: bfloat16 [4, 4096, 3584], P('task', 'tok'), may hold values from -6 to 6
- attn_out: bfloat16 [4, 4096, 3584], P('task', 'tok'), may hold values from -6 to 6
- gain_attn: bfloat16 [3584], replicated, may hold values from 0.5 to 1.5
- gain_mlp: bfloat16 [3584], replicated, may hold values from 0.5 to 1.5
- lengths: int32 [4, 2], P('task'), may hold values from 512 to 2048
Outputs:
- gram_attn: float32 [128, 112, 896], P('tok', 'task')
- gram_mlp: float32 [128, 112, 896], P('tok', 'task')
All inputs are finite; a program needn't handle non-finite values.
Results may differ from a plain program's by a relative error of at most 0.0044.
Values may be sent and summed in bfloat16 or wider, within the bound.
No kernel may reach another device: no remote copies, remote signals or barrier semaphores. Data moves between devices by JAX's collectives and lax.ppermute only.
A program may use at most 64 MiB of HBM per device.

v0:
```python
import jax
import jax.numpy as jnp
from jax import lax
from jax.sharding import PartitionSpec as P


def sent_together(arrays, axis, split_dim, concat_dim, along):
    ends, at = ([], 0)
    for a in arrays[:-1]:
        at += a.shape[along]
        ends.append(at)
    both = jnp.concatenate(arrays, axis=along)
    return tuple(
        jnp.split(
            lax.all_to_all(both, axis, split_axis=split_dim, concat_axis=concat_dim, tiled=True),
            ends,
            axis=along,
        )
    )


def for_sending(value):

    def short(part):
        return part.astype(jnp.bfloat16) if part.dtype == jnp.float32 else part

    return jax.tree.map(short, value)


def from_partner(block, axis, distance):
    count = lax.axis_size(axis)
    route = []
    for low in range(count):
        high = low | 1 << distance
        if high != low and high < count:
            route += [(low, high), (high, low)]
    return lax.ppermute(block, axis, route)


def cut_along(value, dim, length):
    dims = value.shape
    parts = value.reshape(*dims[:dim], length, dims[dim] // length, *dims[dim + 1 :])
    return jnp.moveaxis(parts, dim, 0)


def summed_on_arrival(value, axis, dim):
    parts = cut_along(value, dim, lax.axis_size(axis))
    arrived = lax.all_to_all(parts, axis, split_axis=0, concat_axis=0, tiled=True)
    return arrived.astype(jnp.float32).sum(axis=0)


def normed(values, gain):
    scale = lax.rsqrt(jnp.mean(values * values, axis=-1, keepdims=True) + 1e-06)
    return values * scale * gain.astype(jnp.float32)


def per_device(hidden, attn_out, gain_attn, gain_mlp, lengths):
    tok_dev = hidden.shape[1]
    width = hidden.shape[2]
    n_tok = lax.axis_size("tok")
    n_task = lax.axis_size("task")
    block_side = min(4, max(2, n_tok // 16))
    token_parts = n_tok // (block_side * block_side)
    column_band = width // block_side
    tile_rows = column_band // token_parts
    slice_rows = tok_dev // token_parts
    seq_count = lengths.shape[1]
    seq_slots = tok_dev * n_tok // seq_count
    place = lax.axis_index("tok") * tok_dev + jnp.arange(tok_dev, dtype=jnp.int32)
    which = place // seq_slots
    offset = place % seq_slots
    owner = which[:, None] == jnp.arange(seq_count, dtype=jnp.int32)[None, :]
    limit = jnp.sum(jnp.where(owner, lengths[0][None, :], 0), axis=1)
    live = (offset < limit).astype(jnp.float32)[:, None]
    first = hidden[0].astype(jnp.float32)
    x_attn = (normed(first, gain_attn) * live).astype(jnp.bfloat16)
    mixed = first + attn_out[0].astype(jnp.float32)
    x_mlp = (normed(mixed, gain_mlp) * live).astype(jnp.bfloat16)

    def bands(values):
        split = values.reshape(token_parts, slice_rows, block_side, column_band).transpose(
            2, 0, 1, 3
        )
        shape = (block_side, block_side, token_parts, slice_rows, column_band)
        left_side = jnp.broadcast_to(split[:, None], shape).reshape(n_tok, slice_rows, column_band)
        right_side = jnp.broadcast_to(split[None], shape).reshape(n_tok, slice_rows, column_band)
        return (left_side, right_side)

    left_attn, right_attn = bands(x_attn)
    left_mlp, right_mlp = bands(x_mlp)
    arrived = sent_together((left_attn, right_attn, left_mlp, right_mlp), "tok", 0, 0, 1)
    contract = (((0, 1), (0, 1)), ((), ()))
    tile_attn = lax.dot_general(
        arrived[0], arrived[1], contract, preferred_element_type=jnp.float32
    )
    tile_mlp = lax.dot_general(arrived[2], arrived[3], contract, preferred_element_type=jnp.float32)
    grams = (
        tile_attn.reshape(token_parts, tile_rows, column_band),
        tile_mlp.reshape(token_parts, tile_rows, column_band),
    )
    part_index = lax.axis_index("tok") % token_parts
    depth_bits = token_parts.bit_length() - 1

    def halve(current, bit):
        upper_bit = part_index // (1 << bit) % 2 == 1
        middle = current[0].shape[0] // 2
        outgoing = tuple(
            (jnp.where(upper_bit, piece[:middle], piece[middle:]) for piece in current)
        )
        kept = tuple((jnp.where(upper_bit, piece[middle:], piece[:middle]) for piece in current))
        incoming = jax.tree.map(
            lambda part, own: part.astype(own.dtype),
            from_partner(for_sending(outgoing), "tok", bit),
            outgoing,
        )
        return tuple((mine + theirs for mine, theirs in zip(kept, incoming)))

    grams = halve(grams, depth_bits - 1)
    shaped = tuple(
        (
            piece.reshape(token_parts // 2, n_task, tile_rows // n_task, column_band)
            for piece in grams
        )
    )
    summed = jax.tree.map(lambda part: summed_on_arrival(part, "task", 1), for_sending(shaped))
    grams = tuple(
        (piece.reshape(token_parts // 2, tile_rows // n_task, column_band) for piece in summed)
    )
    for bit in range(depth_bits - 2, -1, -1):
        grams = halve(grams, bit)
    factor = 1.0 / (tok_dev * n_tok)
    final_attn = grams[0] * factor
    final_mlp = grams[1] * factor
    return (final_attn, final_mlp)


def solution(mesh):
    return jax.shard_map(
        per_device,
        mesh=mesh,
        in_specs=(P("task", "tok", None), P("task", "tok", None), P(), P(), P("task", None)),
        out_specs=(P("tok", "task", None), P("tok", "task", None)),
        check_vma=False,
    )
```

profile of v0, /device:TPU:1, one launch (start us, length us, event | category | flops | bytes accessed | tf_op | source)
XLA Modules:
  0.0 219.7 jit_solution(16467990758997533054)
XLA Ops:
  0.6 1.1 reshape.195
  1.7 1.3 multiply_reduce_fusion.1
  3.0 1.1 reshape.197
  4.2 0.7 fusion.17
  5.2 0.7 reshape.196
  5.9 0.7 reshape.198
  6.6 0.4 fusion.6
  7.0 0.1 copy.37
  7.1 0.2 broadcast_in_dim.28
  7.4 0.2 broadcast_in_dim.27
  7.7 0.2 broadcast_in_dim.26
  7.9 0.2 broadcast_in_dim.25
  8.2 4.1 %pad_maximum_fusion = bf16[128,16,896]{2,1,0:T(8,128)(2,1)} fusion(bf16[128,4,896]{2,1,0:T(4,128)(2,1)S(1)} %bitcast.29, bf16[128,4,896]{2,1,0:T(4,128)(2,1)S(1)} %bitcast.30, bf16[128,4,896]{2,1,0:T(4,128)(2,1)S(1)} %bitcast.31, bf16[128,4,896]{2,1,0:T(4,128)(2,1)S(1)} %bitcast.32), kind=kLoop, calls=%fused_computation | loop fusion | flops 14680064 | bytes 7340032 | tf_op jit(solution)/shard_map/concatenate | solution.py:12
  12.3 21.3 %all-to-all-start = ((bf16[128,16,896]{2,1,0:T(8,128)(2,1)}), bf16[128,16,896]{2,1,0:T(8,128)(2,1)}, u32[]{:S(2)}, u32[]{:S(2)}) async-start(bf16[128,16,896]{2,1,0:T(8,128)(2,1)} %pad_maximum_fusion), calls=%async_computation | async-start | bytes 7340032 | tf_op jit(solution)/shard_map/all_to_all | solution.py:15
  33.6 86.6 %all-to-all-done = bf16[128,16,896]{2,1,0:T(8,128)(2,1)} async-done(((bf16[128,16,896]{2,1,0:T(8,128)(2,1)}), bf16[128,16,896]{2,1,0:T(8,128)(2,1)}, u32[]{:S(2)}, u32[]{:S(2)}) %all-to-all-start) | async-done | bytes 3670048 | tf_op jit(solution)/shard_map/all_to_all | solution.py:15
  120.2 4.6 %fusion.18 = (bf16[128,4,896]{2,1,0:T(4,128)(2,1)S(1)}, bf16[128,4,896]{2,1,0:T(4,128)(2,1)S(1)}, bf16[128,4,896]{2,1,0:T(4,128)(2,1)S(1)}, bf16[128,4,896]{2,1,0:T(4,128)(2,1)S(1)}) fusion(bf16[128,16,896]{2,1,0:T(8,128)(2,1)} %all-to-all-done), kind=kLoop, calls=%fused_computation.51 | loop fusion | bytes 7340032 | tf_op jit(solution)/shard_map/split | solution.py:14
  124.8 1.2 convolution_bitcast_fusion
  125.9 0.2 select_convert_fusion
  126.1 0.3 copy.48
  126.4 5.7 %collective-permute-start.3 = (bf16[4,112,896]{2,0,1:T(4,128)(2,1)S(1)}, bf16[4,112,896]{2,0,1:T(4,128)(2,1)S(1)}, u32[]{:S(2)}, u32[]{:S(2)}) collective-permute-start(bf16[4,112,896]{2,0,1:T(4,128)(2,1)S(1)} %copy.48), channel_id=1, source_target_pairs={{0,4},{4,0},{1,5},{5,1},{2,6},{6,2},{3,7},{7,3},{8,12},{12,8},{9,1... | collective-permute-start | bytes 2408456 | tf_op jit(solution)/shard_map/ppermute | solution.py:37
  132.1 1.2 convolution_bitcast_fusion.1
  133.3 0.2 slice_select_fusion
  133.5 14.9 %collective-permute-done.3 = bf16[4,112,896]{2,0,1:T(4,128)(2,1)S(1)} collective-permute-done((bf16[4,112,896]{2,0,1:T(4,128)(2,1)S(1)}, bf16[4,112,896]{2,0,1:T(4,128)(2,1)S(1)}, u32[]{:S(2)}, u32[]{:S(2)}) %collective-permute-start.3) | collective-permute-done | bytes 802848 | tf_op jit(solution)/shard_map/ppermute | solution.py:37
  148.4 1.7 fusion
  150.0 8.7 %all-to-all-start.2 = ((bf16[4,4,1,28,896]{4,1,3,2,0:T(4,128)(2,1)}), bf16[4,4,1,28,896]{4,1,3,2,0:T(4,128)(2,1)}, u32[]{:S(2)}, u32[]{:S(2)}) async-start(bf16[4,4,1,28,896]{4,1,3,2,0:T(4,128)(2,1)} %bitcast.33), calls=%async_computation.2 | async-start | bytes 1605632 | tf_op jit(solution)/shard_map/all_to_all | solution.py:48
  158.8 0.2 select_convert_fusion.1
  158.9 0.3 copy.43
  159.3 3.8 %collective-permute-start = (bf16[4,112,896]{2,0,1:T(4,128)(2,1)S(1)}, bf16[4,112,896]{2,0,1:T(4,128)(2,1)S(1)}, u32[]{:S(2)}, u32[]{:S(2)}) collective-permute-start(bf16[4,112,896]{2,0,1:T(4,128)(2,1)S(1)} %copy.43), channel_id=1, source_target_pairs={{0,4},{4,0},{1,5},{5,1},{2,6},{6,2},{3,7},{7,3},{8,12},{12,8},{9,1... | collective-permute-start | bytes 2408456 | tf_op jit(solution)/shard_map/ppermute | solution.py:37
  163.1 0.2 slice_select_fusion.1
  163.2 16.2 %collective-permute-done = bf16[4,112,896]{2,0,1:T(4,128)(2,1)S(1)} collective-permute-done((bf16[4,112,896]{2,0,1:T(4,128)(2,1)S(1)}, bf16[4,112,896]{2,0,1:T(4,128)(2,1)S(1)}, u32[]{:S(2)}, u32[]{:S(2)}) %collective-permute-start) | collective-permute-done | bytes 802848 | tf_op jit(solution)/shard_map/ppermute | solution.py:37
  179.4 1.7 fusion.1
  181.1 4.3 %all-to-all-start.1 = ((bf16[4,4,1,28,896]{4,1,3,2,0:T(4,128)(2,1)}), bf16[4,4,1,28,896]{4,1,3,2,0:T(4,128)(2,1)S(1)}, u32[]{:S(2)}, u32[]{:S(2)}) async-start(bf16[4,4,1,28,896]{4,1,3,2,0:T(4,128)(2,1)} %bitcast.12), calls=%async_computation.1 | async-start | bytes 1605632 | tf_op jit(solution)/shard_map/all_to_all | solution.py:48
  185.3 1.6 convert_reduce_fusion
  187.0 0.1 select_convert_fusion.2
  187.1 5.5 %collective-permute-start.4 = (bf16[2,28,896]{2,0,1:T(2,128)(2,1)S(1)}, bf16[2,28,896]{2,0,1:T(2,128)(2,1)S(1)}, u32[]{:S(2)}, u32[]{:S(2)}) collective-permute-start(bf16[2,28,896]{2,0,1:T(2,128)(2,1)S(1)} %select_convert_fusion.2), channel_id=1, source_target_pairs={{0,2},{2,0},{1,3},{3,1},{4,6},{6,4},{5,7},{7,5},{8,10},{10,8},{9,1... | collective-permute-start | bytes 301064 | tf_op jit(solution)/shard_map/ppermute | solution.py:37
  192.7 11.0 %all-to-all-done.1 = bf16[4,4,1,28,896]{4,1,3,2,0:T(4,128)(2,1)S(1)} async-done(((bf16[4,4,1,28,896]{4,1,3,2,0:T(4,128)(2,1)}), bf16[4,4,1,28,896]{4,1,3,2,0:T(4,128)(2,1)S(1)}, u32[]{:S(2)}, u32[]{:S(2)}) %all-to-all-start.1) | async-done | bytes 802848 | tf_op jit(solution)/shard_map/all_to_all | solution.py:48
  203.6 0.4 convert_reduce_fusion.1
  204.0 0.1 select_convert_fusion.3
  204.2 7.3 %collective-permute-start.1 = (bf16[2,28,896]{2,0,1:T(2,128)(2,1)S(1)}, bf16[2,28,896]{2,0,1:T(2,128)(2,1)S(1)}, u32[]{:S(2)}, u32[]{:S(2)}) collective-permute-start(bf16[2,28,896]{2,0,1:T(2,128)(2,1)S(1)} %select_convert_fusion.3), channel_id=1, source_target_pairs={{0,2},{2,0},{1,3},{3,1},{4,6},{6,4},{5,7},{7,5},{8,10},{10,8},{9,1... | collective-permute-start | bytes 301064 | tf_op jit(solution)/shard_map/ppermute | solution.py:37
  211.5 0.2 convert_add_fusion
  211.6 0.1 fusion.13
  211.8 3.6 %collective-permute-start.5 = (bf16[1,28,896]{2,0,1:T(2,128)(2,1)S(1)}, bf16[1,28,896]{2,0,1:T(2,128)(2,1)S(1)}, u32[]{:S(2)}, u32[]{:S(2)}) collective-permute-start(bf16[1,28,896]{2,0,1:T(2,128)(2,1)S(1)} %fusion.13), channel_id=1, source_target_pairs={{0,1},{1,0},{2,3},{3,2},{4,5},{5,4},{6,7},{7,6},{8,9},{9,8},{10,11... | collective-permute-start | bytes 150536 | tf_op jit(solution)/shard_map/ppermute | solution.py:37
  215.4 0.1 convert_add_fusion.1
  215.5 0.1 fusion.10
  215.7 2.3 %collective-permute-start.2 = (bf16[1,28,896]{2,0,1:T(2,128)(2,1)S(1)}, bf16[1,28,896]{2,0,1:T(2,128)(2,1)S(1)}, u32[]{:S(2)}, u32[]{:S(2)}) collective-permute-start(bf16[1,28,896]{2,0,1:T(2,128)(2,1)S(1)} %fusion.10), channel_id=1, source_target_pairs={{0,1},{1,0},{2,3},{3,2},{4,5},{5,4},{6,7},{7,6},{8,9},{9,8},{10,11... | collective-permute-start | bytes 150536 | tf_op jit(solution)/shard_map/ppermute | solution.py:37
  217.9 0.8 fusion.12
  218.8 0.1 collective-permute-done.2
  218.9 0.8 fusion.9
  (11 shorter events, 0.4 us)
Async XLA Ops:
  12.3 107.9 %all-to-all-start = ((bf16[128,16,896]{2,1,0:T(8,128)(2,1)}), bf16[128,16,896]{2,1,0:T(8,128)(2,1)}, u32[]{:S(2)}, u32[]{:S(2)}) async-start(bf16[128,16,896]{2,1,0:T(8,128)(2,1)} %pad_maximum_fusion), calls=%async_computation | async-start | bytes 7340032 | tf_op jit(solution)/shard_map/all_to_all | solution.py:15
  126.4 21.9 %collective-permute-start.3 = (bf16[4,112,896]{2,0,1:T(4,128)(2,1)S(1)}, bf16[4,112,896]{2,0,1:T(4,128)(2,1)S(1)}, u32[]{:S(2)}, u32[]{:S(2)}) collective-permute-start(bf16[4,112,896]{2,0,1:T(4,128)(2,1)S(1)} %copy.48), channel_id=1, source_target_pairs={{0,4},{4,0},{1,5},{5,1},{2,6},{6,2},{3,7},{7,3},{8,12},{12,8},{9,1... | collective-permute-start | bytes 2408456 | tf_op jit(solution)/shard_map/ppermute | solution.py:37
  150.0 31.0 %all-to-all-start.2 = ((bf16[4,4,1,28,896]{4,1,3,2,0:T(4,128)(2,1)}), bf16[4,4,1,28,896]{4,1,3,2,0:T(4,128)(2,1)}, u32[]{:S(2)}, u32[]{:S(2)}) async-start(bf16[4,4,1,28,896]{4,1,3,2,0:T(4,128)(2,1)} %bitcast.33), calls=%async_computation.2 | async-start | bytes 1605632 | tf_op jit(solution)/shard_map/all_to_all | solution.py:48
  159.3 20.1 %collective-permute-start = (bf16[4,112,896]{2,0,1:T(4,128)(2,1)S(1)}, bf16[4,112,896]{2,0,1:T(4,128)(2,1)S(1)}, u32[]{:S(2)}, u32[]{:S(2)}) collective-permute-start(bf16[4,112,896]{2,0,1:T(4,128)(2,1)S(1)} %copy.43), channel_id=1, source_target_pairs={{0,4},{4,0},{1,5},{5,1},{2,6},{6,2},{3,7},{7,3},{8,12},{12,8},{9,1... | collective-permute-start | bytes 2408456 | tf_op jit(solution)/shard_map/ppermute | solution.py:37
  181.1 22.5 %all-to-all-start.1 = ((bf16[4,4,1,28,896]{4,1,3,2,0:T(4,128)(2,1)}), bf16[4,4,1,28,896]{4,1,3,2,0:T(4,128)(2,1)S(1)}, u32[]{:S(2)}, u32[]{:S(2)}) async-start(bf16[4,4,1,28,896]{4,1,3,2,0:T(4,128)(2,1)} %bitcast.12), calls=%async_computation.1 | async-start | bytes 1605632 | tf_op jit(solution)/shard_map/all_to_all | solution.py:48
  187.1 24.3 %collective-permute-start.4 = (bf16[2,28,896]{2,0,1:T(2,128)(2,1)S(1)}, bf16[2,28,896]{2,0,1:T(2,128)(2,1)S(1)}, u32[]{:S(2)}, u32[]{:S(2)}) collective-permute-start(bf16[2,28,896]{2,0,1:T(2,128)(2,1)S(1)} %select_convert_fusion.2), channel_id=1, source_target_pairs={{0,2},{2,0},{1,3},{3,1},{4,6},{6,4},{5,7},{7,5},{8,10},{10,8},{9,1... | collective-permute-start | bytes 301064 | tf_op jit(solution)/shard_map/ppermute | solution.py:37
  204.2 11.2 %collective-permute-start.1 = (bf16[2,28,896]{2,0,1:T(2,128)(2,1)S(1)}, bf16[2,28,896]{2,0,1:T(2,128)(2,1)S(1)}, u32[]{:S(2)}, u32[]{:S(2)}) collective-permute-start(bf16[2,28,896]{2,0,1:T(2,128)(2,1)S(1)} %select_convert_fusion.3), channel_id=1, source_target_pairs={{0,2},{2,0},{1,3},{3,1},{4,6},{6,4},{5,7},{7,5},{8,10},{10,8},{9,1... | collective-permute-start | bytes 301064 | tf_op jit(solution)/shard_map/ppermute | solution.py:37
  211.8 6.2 %collective-permute-start.5 = (bf16[1,28,896]{2,0,1:T(2,128)(2,1)S(1)}, bf16[1,28,896]{2,0,1:T(2,128)(2,1)S(1)}, u32[]{:S(2)}, u32[]{:S(2)}) collective-permute-start(bf16[1,28,896]{2,0,1:T(2,128)(2,1)S(1)} %fusion.13), channel_id=1, source_target_pairs={{0,1},{1,0},{2,3},{3,2},{4,5},{5,4},{6,7},{7,6},{8,9},{9,8},{10,11... | collective-permute-start | bytes 150536 | tf_op jit(solution)/shard_map/ppermute | solution.py:37
  215.7 3.2 %collective-permute-start.2 = (bf16[1,28,896]{2,0,1:T(2,128)(2,1)S(1)}, bf16[1,28,896]{2,0,1:T(2,128)(2,1)S(1)}, u32[]{:S(2)}, u32[]{:S(2)}) collective-permute-start(bf16[1,28,896]{2,0,1:T(2,128)(2,1)S(1)} %fusion.10), channel_id=1, source_target_pairs={{0,1},{1,0},{2,3},{3,2},{4,5},{5,4},{6,7},{7,6},{8,9},{9,8},{10,11... | collective-permute-start | bytes 150536 | tf_op jit(solution)/shard_map/ppermute | solution.py:37
where the time goes:
time: 221 us; the launch traced here: 220 us
  waiting for transfers between devices  129 us (58%)
  starting transfers between devices  62.4 us (28%)
  other arithmetic  15 us (7%)
  local copies, waits for them, and re-layouts  10.2 us (5%)
  matrix products  2.3 us (1%)
    all_to_all x1, waiting for transfers between devices, sent_together(): lax.all_to_all(both, axis, split_axis=split_dim, concat_axis=concat_dim,...  86.6 us
    ppermute x6, waiting for transfers between devices, from_partner(): return lax.ppermute(block, axis, route)  31.1 us
    ppermute x6, starting transfers between devices, from_partner(): return lax.ppermute(block, axis, route)  28.2 us
    all_to_all x1, starting transfers between devices, sent_together(): lax.all_to_all(both, axis, split_axis=split_dim, concat_axis=concat_dim,...  21.3 us
    all_to_all x2, starting transfers between devices, summed_on_arrival(): lax.all_to_all(parts, axis, split_axis=0, concat_axis=0, tiled=True)  13 us
    all_to_all x2, waiting for transfers between devices, summed_on_arrival(): lax.all_to_all(parts, axis, split_axis=0, concat_axis=0, tiled=True)  11 us
    split x1, local copies, waits for them, and re-layouts, sent_together(): jnp.split(lax.all_to_all(both, axis, split_axis=split_dim, concat_axis=co...  4.57 us
  transfers between devices with their start and end apart: 9, of which 5 were waited for; matrix products, arithmetic and copies ran while one was open for 3% of the time, Pallas kernels for 0%

commit v1 on v0

v1 whole, which is shorter than its diff:
```python
import jax
import jax.numpy as jnp
from jax import lax
from jax.sharding import Mesh
from jax.sharding import PartitionSpec as P

TOK = ("z", "yh", "x", "core")
YRING = ("yh", "task")


def normed(values, gain):
    scale = lax.rsqrt(jnp.mean(values * values, axis=-1, keepdims=True) + 1e-06)
    return values * scale * gain.astype(jnp.float32)


def per_device(hidden, attn_out, gain_attn, gain_mlp, lengths):
    rows = hidden.shape[1]
    width = hidden.shape[2]
    n_z, n_yh, n_x, n_core = (lax.axis_size(a) for a in TOK)
    n_task = lax.axis_size("task")
    tokens = rows * n_z * n_yh * n_x * n_core
    seq_len = tokens // lengths.shape[1]
    band = width // 4
    part = band // (n_x * n_core * n_task)
    z = lax.axis_index("z")
    core = lax.axis_index("core")

    place = lax.axis_index(TOK) * rows + jnp.arange(rows, dtype=jnp.int32)
    which = lax.axis_index(TOK) * rows // seq_len
    limit = lax.dynamic_index_in_dim(lengths[0], which, keepdims=False)
    live = (place - which * seq_len < limit).astype(jnp.float32)[:, None]
    first = hidden[0].astype(jnp.float32)
    x_attn = (normed(first, gain_attn) * live).astype(jnp.bfloat16)
    mixed = first + attn_out[0].astype(jnp.float32)
    x_mlp = (normed(mixed, gain_mlp) * live).astype(jnp.bfloat16)

    both = jnp.concatenate([x_attn, x_mlp], axis=1)
    seen = lax.all_gather(both, ("z", "core"), axis=0, tiled=True)

    def tile(at):
        left = lax.dynamic_slice_in_dim(seen, at * width + z // 2 * band, band, 1)
        right = lax.dynamic_slice_in_dim(seen, at * width + z % 2 * 2 * band, 2 * band, 1)
        full = lax.dot_general(
            left, right, (((0,), (0,)), ((), ())), preferred_element_type=jnp.float32
        )
        full = full.reshape(n_x, n_core, n_task, part, n_yh, band)
        return jnp.where(core == 0, full[:, 0], full[:, 1])

    parts = jnp.stack([tile(0), tile(1)])
    parts = parts.transpose(4, 2, 1, 0, 3, 5).astype(jnp.bfloat16)
    parts = parts.reshape(n_yh * n_task * n_x * 2 * part, band)
    ring = lax.psum_scatter(parts, YRING, scatter_dimension=0, tiled=True)
    ring = ring.reshape(n_x, 2 * part, band)
    ring = lax.all_to_all(ring, "x", split_axis=0, concat_axis=0, tiled=True)
    total = ring.astype(jnp.float32).sum(axis=0) * (1.0 / tokens)
    return total[None, :part], total[None, part:]


def solution(mesh):
    n_task = mesh.shape["task"]
    grid = Mesh(mesh.devices.reshape(n_task, 8, 2, 4, 2), ("task",) + TOK)
    return jax.shard_map(
        per_device,
        mesh=grid,
        in_specs=(P("task", TOK, None), P("task", TOK, None), P(), P(), P("task", None)),
        out_specs=(P(TOK, "task", None), P(TOK, "task", None)),
        check_vma=False,
    )
```

time: 221 us -> 180 us (0.81)
  the two profiles are of different devices: /device:TPU:1 before, /device:TPU:24 now
where the time goes in v1:
time: 180 us; the launch traced here: 179 us
  waiting for transfers between devices  106 us (59%)
  local copies, waits for them, and re-layouts  27.3 us (15%)
  between operations  14.2 us (8%)
  blocking collectives  11.7 us (6%)
  matrix products  10.8 us (6%)
  other arithmetic  8.75 us (5%)
    all_gather x1, waiting for transfers between devices, per_device(): seen = lax.all_gather(both, ('z', 'core'), axis=0, tiled=True)  58.8 us
    reduce_scatter x1, waiting for transfers between devices, per_device(): ring = lax.psum_scatter(parts, YRING, scatter_dimension=0, tiled=True)  47.7 us
    reshape x2, local copies, waits for them, and re-layouts, tile(): full = full.reshape(n_x, n_core, n_task, part, n_yh, band)  13 us
    all_to_all x1, blocking collectives, per_device(): ring = lax.all_to_all(ring, 'x', split_axis=0, concat_axis=0, tiled=True)  11.7 us
    dot_general x2, matrix products, tile(): lax.dot_general(left, right, (((0,), (0,)), ((), ())), preferred_element_...  10.8 us
    slice x2, local copies, waits for them, and re-layouts, tile(): return jnp.where(core == 0, full[:, 0], full[:, 1])  6.31 us
    reshape x1, local copies, waits for them, and re-layouts, per_device(): parts = parts.reshape(n_yh * n_task * n_x * 2 * part, band)  6 us
  transfers between devices with their start and end apart: 2, of which 2 were waited for; matrix products, arithmetic and copies ran while one was open for 0% of the time, Pallas kernels for 0%

profile of v1, /device:TPU:24, one launch (start us, length us, event | category | flops | bytes accessed | tf_op | source)
XLA Modules:
  0.0 179.4 jit_solution(12961962622690158551)
XLA Ops:
  7.2 0.0 copy-start
  7.2 0.0 all-gather.2.cloned.1.call-start
  7.3 0.7 convert_element_type.40
  8.0 0.7 convert_element_type.45
  8.7 0.0 copy-done
  8.7 0.6 constant_dynamic-slice_fusion
  9.2 0.6 compare_convert_fusion
  9.9 1.3 fusion.10
  11.2 1.3 fusion.13
  12.4 0.8 pad_maximum_fusion
  13.2 0.0 all-gather.2.cloned.1.call-update
  13.2 0.0 reduce-scatter.2.cloned.1.call-start
  13.3 58.8 %all-gather.2.cloned.1.call-done = bf16[512,7168]{1,0:T(8,128)(2,1)} async-done(((bf16[32,7168]{1,0:T(8,128)(2,1)}), bf16[512,7168]{1,0:T(8,128)(2,1)}) %all-gather.2.cloned.1.call-update) | async-done | bytes 7340048 | tf_op jit(solution)/shard_map/all_gather | solution.py:38
  72.1 5.4 %fusion.4 = bf16[896,1792]{1,0:T(8,128)(2,1)} fusion(bf16[512,7168]{1,0:T(8,128)(2,1)} %all-gather.2.cloned.1.call-done, s32[]{:T(128)S(6)} %select_n.75, s32[]{:T(128)S(6)} %select_n.74), kind=kOutput, calls=%fused_computation.7 | convolution fusion | flops 1644167168 | bytes 5963784 | tf_op jit(solution)/shard_map/dot_general | solution.py:43
  77.5 5.9 %reshape.88 = bf16[4,2,4,28,2,896]{5,4,3,2,1,0:T(2,128)(2,1)S(1)} reshape(bf16[896,1792]{1,0:T(8,128)(2,1)} %fusion.4) | data formatting | bytes 6422528 | tf_op jit(solution)/shard_map/reshape | solution.py:46
  83.5 5.4 %fusion.6 = bf16[896,1792]{1,0:T(8,128)(2,1)} fusion(bf16[512,7168]{1,0:T(8,128)(2,1)} %all-gather.2.cloned.1.call-done, s32[]{:T(128)S(6)} %select_n.71, s32[]{:T(128)S(6)} %select_n.69), kind=kOutput, calls=%fused_computation.9 | convolution fusion | flops 1644167168 | bytes 5963784 | tf_op jit(solution)/shard_map/dot_general | solution.py:43
  88.9 7.1 %reshape.87 = bf16[4,2,4,28,2,896]{5,4,3,2,1,0:T(2,128)(2,1)} reshape(bf16[896,1792]{1,0:T(8,128)(2,1)} %fusion.6) | data formatting | bytes 6422528 | tf_op jit(solution)/shard_map/reshape | solution.py:46
  96.0 4.1 %fusion.16 = (bf16[4,1,4,28,2,896]{5,4,3,2,1,0:T(2,128)(2,1)S(1)}, bf16[4,1,4,28,2,896]{5,4,3,2,1,0:T(2,128)(2,1)S(1)}) fusion(bf16[4,2,4,28,2,896]{5,4,3,2,1,0:T(2,128)(2,1)} %reshape.87), kind=kLoop, calls=%fused_computation.31 | loop fusion | bytes 6422528 | tf_op jit(solution)/shard_map/slice | solution.py:47
  100.1 2.2 %fusion.17 = (bf16[4,1,4,28,2,896]{5,4,3,2,1,0:T(2,128)(2,1)S(1)}, bf16[4,1,4,28,2,896]{5,4,3,2,1,0:T(2,128)(2,1)S(1)}) fusion(bf16[4,2,4,28,2,896]{5,4,3,2,1,0:T(2,128)(2,1)S(1)} %reshape.88), kind=kLoop, calls=%fused_computation.32 | loop fusion | bytes 6422528 | tf_op jit(solution)/shard_map/slice | solution.py:47
  102.3 0.5 fusion.2
  102.8 0.5 fusion.3
  103.3 2.3 %maximum_bitcast_fusion = bf16[2,4,4,2,28,896]{5,4,3,2,1,0:T(8,128)(2,1)} fusion(bf16[1,4,4,28,2,896]{5,3,0,1,2,4:T(8,128)(2,1)S(1)} %fusion.3, bf16[1,4,4,28,2,896]{5,3,0,1,2,4:T(8,128)(2,1)S(1)} %fusion.2), kind=kLoop, calls=%fused_computation | loop fusion | flops 1605632 | bytes 6422528 | tf_op jit(solution)/shard_map/convert_element_type | solution.py:50
  105.6 6.0 %reshape.89 = bf16[1792,896]{1,0:T(8,128)(2,1)} reshape(bf16[2,4,4,2,28,896]{5,4,3,2,1,0:T(8,128)(2,1)} %maximum_bitcast_fusion) | data formatting | bytes 6422528 | tf_op jit(solution)/shard_map/reshape | solution.py:51
  111.6 0.0 reduce-scatter.2.cloned.1.call-update
  111.6 47.7 %reduce-scatter.2.cloned.1.call-done = bf16[224,896]{1,0:T(8,128)(2,1)} async-done(((bf16[1792,896]{1,0:T(8,128)(2,1)}), bf16[224,896]{1,0:T(8,128)(2,1)}) %reduce-scatter.2.cloned.1.call-update) | async-done | bytes 401424 | tf_op jit(solution)/shard_map/reduce_scatter | solution.py:52
  159.3 11.7 %all_to_all.5 = bf16[4,56,896]{2,1,0:T(8,128)(2,1)S(1)} all-to-all(bf16[4,56,896]{2,1,0:T(8,128)(2,1)} %bitcast.20), channel_id=1, replica_groups=mesh['task'=4,'z'=8,'yh'=2,'x'=4,'core'=2] {'x'}, dimensions={0} | all-to-all | bytes 802816 | tf_op jit(solution)/shard_map/all_to_all | solution.py:54
  171.0 0.1 convert_reduce_fusion
  171.1 0.7 broadcast_in_dim.5
  171.8 0.7 broadcast_in_dim.4
  (3 shorter events, 0.0 us)
Async XLA Ops:
  7.2 1.5 copy-start
  7.2 64.9 %all-gather.2.cloned.1.call-start = ((), (), s32[]{:S(2)}) async-start(), calls=%async_computation.2 | async-start | bytes 7798784 | tf_op jit(solution)/shard_map/all_gather | solution.py:38
  13.2 146.0 %reduce-scatter.2.cloned.1.call-start = ((), (), s32[]{:S(2)}) async-start(), calls=%async_computation.3 | async-start | bytes 3612672 | tf_op jit(solution)/shard_map/reduce_scatter | solution.py:52
Sparse Core Ops, SparseCore 0:
  13.4 58.7 all-gather.1
  111.7 47.4 reduce-scatter.1

commit v2 on v1

v2 whole, which is shorter than its diff:
```python
import jax
import jax.numpy as jnp
import numpy as np
from jax import lax
from jax.sharding import Mesh
from jax.sharding import PartitionSpec as P

TOK = ("z", "yh", "x", "core")
ALL = ("task",) + TOK
YRING = ("yh", "task")
PAIRS = ((0, 1), (0, 2), (0, 3), (1, 2), (1, 3), (2, 3), (0, 1), (2, 3))
MIXED = 6


def tile_of(pair, core):
    i, j = PAIRS[pair]
    if pair < MIXED:
        return (i, j) if core == 0 else (j, i)
    return (i, i) if core == 0 else (j, j)


def home_routes(shape):
    flat = np.arange(np.prod(shape)).reshape(shape)
    by_z, by_y = [], []
    for t, z, yh, x, core in np.ndindex(*shape):
        here = int(flat[t, z, yh, x, core])
        i, j = tile_of(z, core)
        by_z.append((here, int(flat[t, 2 * i + j // 2, j % 2, x, yh])))
        i, j = tile_of(yh * shape[0] + t, core)
        by_y.append((here, int(flat[z % 4, 2 * i + j // 2, j % 2, x, z // 4])))
    return by_z, by_y


def normed(values, gain):
    scale = lax.rsqrt(jnp.mean(values * values, axis=-1, keepdims=True) + 1e-06)
    return values * scale * gain.astype(jnp.float32)


def solution(mesh):
    shape = (mesh.shape["task"], 8, 2, 4, 2)
    grid = Mesh(mesh.devices.reshape(shape), ALL)
    by_z, by_y = home_routes(shape)

    def per_device(hidden, attn_out, gain_attn, gain_mlp, lengths):
        rows = hidden.shape[1]
        width = hidden.shape[2]
        n_x = lax.axis_size("x")
        tokens = rows * lax.axis_size(TOK)
        seq_len = tokens // lengths.shape[1]
        band = width // 4
        core = lax.axis_index("core")

        start = lax.axis_index(TOK) * rows
        which = start // seq_len
        limit = lax.dynamic_index_in_dim(lengths[0], which, keepdims=False)
        place = start - which * seq_len + jnp.arange(rows, dtype=jnp.int32)
        live = (place < limit).astype(jnp.float32)[:, None]
        first = hidden[0].astype(jnp.float32)
        x_attn = (normed(first, gain_attn) * live).astype(jnp.bfloat16)
        mixed = first + attn_out[0].astype(jnp.float32)
        x_mlp = (normed(mixed, gain_mlp) * live).astype(jnp.bfloat16)

        def spread(values, ring):
            cut = [values[:, b * band : (b + 1) * band] for b in range(4)]
            out = jnp.stack([jnp.concatenate([cut[i], cut[j]], axis=1) for i, j in PAIRS])
            return lax.all_to_all(out, ring, split_axis=0, concat_axis=0, tiled=True)

        def tile(own, pair):
            own = own.reshape(-1, 2 * band)
            other = lax.ppermute(own, "core", [(0, 1), (1, 0)])
            side = jnp.where((core == 0) == (pair < MIXED), 1, 0)

            def product(seen):
                left = lax.dynamic_slice_in_dim(seen, core * band, band, 1)
                right = lax.dynamic_slice_in_dim(seen, side * band, band, 1)
                return lax.dot_general(
                    left, right, (((0,), (0,)), ((), ())), preferred_element_type=jnp.float32
                )

            return (product(own) + product(other)).astype(jnp.bfloat16)

        def reduced(part, ring, count):
            part = part.reshape(count, -1, band)
            got = lax.all_to_all(part, ring, split_axis=0, concat_axis=0, tiled=True)
            return got.astype(jnp.float32).sum(axis=0)

        got_attn = spread(x_attn, "z")
        got_mlp = spread(x_mlp, YRING)
        part_attn = tile(got_attn, lax.axis_index("z"))
        part_mlp = tile(got_mlp, lax.axis_index(YRING))
        half_attn = reduced(part_attn, "x", n_x).astype(jnp.bfloat16)
        half_mlp = reduced(part_mlp, "x", n_x).astype(jnp.bfloat16)
        scale = 1.0 / tokens
        end_attn = (reduced(half_attn, YRING, 8) * scale).astype(jnp.bfloat16)
        end_mlp = (reduced(half_mlp, "z", 8) * scale).astype(jnp.bfloat16)
        home_attn = lax.ppermute(end_attn, ALL, by_z)
        home_mlp = lax.ppermute(end_mlp, ALL, by_y)
        return home_attn.astype(jnp.float32)[None], home_mlp.astype(jnp.float32)[None]

    return jax.shard_map(
        per_device,
        mesh=grid,
        in_specs=(P("task", TOK, None), P("task", TOK, None), P(), P(), P("task", None)),
        out_specs=(P(TOK, "task", None), P(TOK, "task", None)),
        check_vma=False,
    )
```

time: 180 us -> 183 us (1.017)
  the two profiles are of different devices: /device:TPU:24 before, /device:TPU:1 now
where the time goes in v2:
time: 183 us; the launch traced here: 182 us
  waiting for transfers between devices  102 us (56%)
  starting transfers between devices  51.5 us (28%)
  local copies, waits for them, and re-layouts  11.2 us (6%)
  other arithmetic  10.2 us (6%)
  matrix products  6.22 us (3%)
    all_to_all x4, waiting for transfers between devices, reduced(): got = lax.all_to_all(part, ring, split_axis=0, concat_axis=0, tiled=True)  55.5 us
    all_to_all x2, waiting for transfers between devices, spread(): return lax.all_to_all(out, ring, split_axis=0, concat_axis=0, tiled=True)  42.8 us
    all_to_all x2, starting transfers between devices, spread(): return lax.all_to_all(out, ring, split_axis=0, concat_axis=0, tiled=True)  19.8 us
    all_to_all x4, starting transfers between devices, reduced(): got = lax.all_to_all(part, ring, split_axis=0, concat_axis=0, tiled=True)  14.5 us
    ppermute x1, starting transfers between devices, per_device(): home_attn = lax.ppermute(end_attn, ALL, by_z)  7.84 us
    dot_general x4, matrix products, product(): lax.dot_general(left, right, (((0,), (0,)), ((), ())), preferred_element_...  6.22 us
    unnamed x10, local copies, waits for them, and re-layouts  5.19 us
    ppermute x2, starting transfers between devices, tile(): other = lax.ppermute(own, 'core', [(0, 1), (1, 0)])  5.06 us
  transfers between devices with their start and end apart: 10, of which 7 were waited for; matrix products, arithmetic and copies ran while one was open for 9% of the time, Pallas kernels for 0%

profile of v2, /device:TPU:1, one launch (start us, length us, event | category | flops | bytes accessed | tf_op | source)
XLA Modules:
  0.0 182.2 jit_solution(3154322518169001445)
XLA Ops:
  0.7 0.7 convert_element_type.57
  1.4 0.7 convert_element_type.65
  2.1 0.6 constant_dynamic-slice_fusion
  2.7 0.6 compare_convert_fusion
  3.3 1.3 multiply_reduce_fusion
  4.6 1.3 multiply_convert_fusion
  5.9 0.6 fusion.32
  6.5 0.7 fusion.17
  7.2 0.7 fusion.19
  7.8 0.7 fusion.26
  8.5 0.7 fusion.15
  9.2 0.7 fusion.34
  9.8 0.7 fusion.33
  10.5 0.7 fusion.35
  11.1 7.6 %all-to-all-start.3 = ((bf16[8,32,1792]{2,1,0:T(8,128)(2,1)}), bf16[8,32,1792]{2,1,0:T(8,128)(2,1)S(1)}, u32[]{:S(2)}, u32[]{:S(2)}) async-start(bf16[8,32,1792]{2,1,0:T(8,128)(2,1)} %fusion.35), calls=%async_computation.3 | async-start | bytes 1835008 | tf_op jit(solution)/shard_map/all_to_all | solution.py:66
  18.8 0.6 fusion.28
  19.4 0.6 fusion.23
  20.1 0.7 fusion.25
  20.7 0.6 fusion.27
  21.4 0.7 fusion.21
  22.0 0.6 fusion.30
  22.7 0.6 fusion.29
  23.3 0.7 fusion.31
  24.0 19.1 %all-to-all-done.3 = bf16[8,32,1792]{2,1,0:T(8,128)(2,1)S(1)} async-done(((bf16[8,32,1792]{2,1,0:T(8,128)(2,1)}), bf16[8,32,1792]{2,1,0:T(8,128)(2,1)S(1)}, u32[]{:S(2)}, u32[]{:S(2)}) %all-to-all-start.3) | async-done | bytes 917536 | tf_op jit(solution)/shard_map/all_to_all | solution.py:66
  43.1 12.1 %all-to-all-start = ((bf16[8,32,1792]{2,1,0:T(8,128)(2,1)}), bf16[8,32,1792]{2,1,0:T(8,128)(2,1)S(1)}, u32[]{:S(2)}, u32[]{:S(2)}) async-start(bf16[8,32,1792]{2,1,0:T(8,128)(2,1)} %fusion.31), calls=%async_computation | async-start | bytes 1835008 | tf_op jit(solution)/shard_map/all_to_all | solution.py:66
  55.2 2.7 %collective-permute-start.2 = (bf16[256,1792]{1,0:T(8,128)(2,1)S(1)}, bf16[256,1792]{1,0:T(8,128)(2,1)S(1)}, u32[]{:S(2)}, u32[]{:S(2)}) collective-permute-start(bf16[256,1792]{1,0:T(8,128)(2,1)S(1)} %bitcast.72), channel_id=1, source_target_pairs={{0,1},{1,0},{2,3},{3,2},{4,5},{5,4},{6,7},{7,6},{8,9},{9,8},{10,11... | collective-permute-start | bytes 2752520 | tf_op jit(solution)/shard_map/ppermute | solution.py:70
  57.9 23.7 %all-to-all-done = bf16[8,32,1792]{2,1,0:T(8,128)(2,1)S(1)} async-done(((bf16[8,32,1792]{2,1,0:T(8,128)(2,1)}), bf16[8,32,1792]{2,1,0:T(8,128)(2,1)S(1)}, u32[]{:S(2)}, u32[]{:S(2)}) %all-to-all-start) | async-done | bytes 917536 | tf_op jit(solution)/shard_map/all_to_all | solution.py:66
  81.6 2.4 %collective-permute-start = (bf16[256,1792]{1,0:T(8,128)(2,1)S(1)}, bf16[256,1792]{1,0:T(8,128)(2,1)}, u32[]{:S(2)}, u32[]{:S(2)}) collective-permute-start(bf16[256,1792]{1,0:T(8,128)(2,1)S(1)} %bitcast.74), channel_id=1, source_target_pairs={{0,1},{1,0},{2,3},{3,2},{4,5},{5,4},{6,7},{7,6},{8,9},{9,8},{10,11... | collective-permute-start | bytes 2752520 | tf_op jit(solution)/shard_map/ppermute | solution.py:70
  84.0 0.7 fusion.6
  84.7 1.9 %add_convert_fusion = bf16[896,896]{1,0:T(8,128)(2,1)} fusion(f32[896,896]{1,0:T(8,128)S(1)} %fusion.6, bf16[256,1792]{1,0:T(8,128)(2,1)S(1)} %collective-permute-done.2, s32[]{:T(128)S(6)} %select_n.36, s32[]{:T(128)S(6)} %select_n.32), kind=kOutput, calls=%fused_computation | convolution fusion | flops 412647424 | bytes 5734408 | tf_op jit(solution)/shard_map/dot_general | solution.py:76
  86.5 4.0 %all-to-all-start.4 = ((bf16[4,224,896]{2,1,0:T(8,128)(2,1)}), bf16[4,224,896]{2,1,0:T(8,128)(2,1)S(1)}, u32[]{:S(2)}, u32[]{:S(2)}) async-start(bf16[4,224,896]{2,1,0:T(8,128)(2,1)} %bitcast.19), calls=%async_computation.4 | async-start | bytes 3211264 | tf_op jit(solution)/shard_map/all_to_all | solution.py:84
  90.5 0.7 fusion.11
  91.2 3.0 %add_convert_fusion.1 = bf16[896,896]{1,0:T(8,128)(2,1)} fusion(f32[896,896]{1,0:T(8,128)S(1)} %fusion.11, bf16[256,1792]{1,0:T(8,128)(2,1)} %collective-permute-done, s32[]{:T(128)S(6)} %select_n.34, s32[]{:T(128)S(6)} %select_n.32), kind=kOutput, calls=%fused_computation.1 | convolution fusion | flops 412647424 | bytes 5734408 | tf_op jit(solution)/shard_map/dot_general | solution.py:76
  94.2 17.2 %all-to-all-done.4 = bf16[4,224,896]{2,1,0:T(8,128)(2,1)S(1)} async-done(((bf16[4,224,896]{2,1,0:T(8,128)(2,1)}), bf16[4,224,896]{2,1,0:T(8,128)(2,1)S(1)}, u32[]{:S(2)}, u32[]{:S(2)}) %all-to-all-start.4) | async-done | bytes 1605664 | tf_op jit(solution)/shard_map/all_to_all | solution.py:84
  111.4 3.6 %all-to-all-start.1 = ((bf16[4,224,896]{2,1,0:T(8,128)(2,1)}), bf16[4,224,896]{2,1,0:T(8,128)(2,1)S(1)}, u32[]{:S(2)}, u32[]{:S(2)}) async-start(bf16[4,224,896]{2,1,0:T(8,128)(2,1)} %bitcast.71), calls=%async_computation.1 | async-start | bytes 3211264 | tf_op jit(solution)/shard_map/all_to_all | solution.py:84
  115.0 1.1 reduce_sum.64
  116.1 1.8 %reshape.57 = bf16[8,28,896]{2,1,0:T(8,128)(2,1)} reshape(bf16[224,896]{1,0:T(8,128)(2,1)} %reduce_sum.64) | data formatting | bytes 802816 | tf_op jit(solution)/shard_map/reshape | solution.py:83
  117.9 17.0 %all-to-all-done.1 = bf16[4,224,896]{2,1,0:T(8,128)(2,1)S(1)} async-done(((bf16[4,224,896]{2,1,0:T(8,128)(2,1)}), bf16[4,224,896]{2,1,0:T(8,128)(2,1)S(1)}, u32[]{:S(2)}, u32[]{:S(2)}) %all-to-all-start.1) | async-done | bytes 1605664 | tf_op jit(solution)/shard_map/all_to_all | solution.py:84
  134.9 3.5 %all-to-all-start.5 = ((bf16[8,28,896]{2,1,0:T(8,128)(2,1)}), bf16[8,28,896]{2,1,0:T(8,128)(2,1)S(1)}, u32[]{:S(2)}, u32[]{:S(2)}) async-start(bf16[8,28,896]{2,1,0:T(8,128)(2,1)} %reshape.57), calls=%async_computation.5 | async-start | bytes 917504 | tf_op jit(solution)/shard_map/all_to_all | solution.py:84
  138.9 0.8 reshape.54
  139.7 12.8 %all-to-all-done.5 = bf16[8,28,896]{2,1,0:T(8,128)(2,1)S(1)} async-done(((bf16[8,28,896]{2,1,0:T(8,128)(2,1)}), bf16[8,28,896]{2,1,0:T(8,128)(2,1)S(1)}, u32[]{:S(2)}, u32[]{:S(2)}) %all-to-all-start.5) | async-done | bytes 401440 | tf_op jit(solution)/shard_map/all_to_all | solution.py:84
  152.5 3.5 %all-to-all-start.2 = ((bf16[8,28,896]{2,1,0:T(8,128)(2,1)}), bf16[8,28,896]{2,1,0:T(8,128)(2,1)S(1)}, u32[]{:S(2)}, u32[]{:S(2)}) async-start(bf16[8,28,896]{2,1,0:T(8,128)(2,1)} %reshape.54), calls=%async_computation.2 | async-start | bytes 917504 | tf_op jit(solution)/shard_map/all_to_all | solution.py:84
  156.1 4.3 %collective-permute-start.3 = (bf16[28,896]{1,0:T(8,128)(2,1)S(1)}, bf16[28,896]{1,0:T(8,128)(2,1)S(1)}, u32[]{:S(2)}, u32[]{:S(2)}) collective-permute-start(bf16[28,896]{1,0:T(8,128)(2,1)S(1)} %multiply_convert_fusion.1), channel_id=1, source_target_pairs={{0,8},{1,32},{2,10},{3,34},{4,12},{5,36},{6,14},{7,38},{8,56},{9,1... | collective-permute-start | bytes 150536 | tf_op jit(solution)/shard_map/ppermute | solution.py:97
  160.5 8.4 %all-to-all-done.2 = bf16[8,28,896]{2,1,0:T(8,128)(2,1)S(1)} async-done(((bf16[8,28,896]{2,1,0:T(8,128)(2,1)}), bf16[8,28,896]{2,1,0:T(8,128)(2,1)S(1)}, u32[]{:S(2)}, u32[]{:S(2)}) %all-to-all-start.2) | async-done | bytes 401440 | tf_op jit(solution)/shard_map/all_to_all | solution.py:84
  169.0 7.8 %collective-permute-start.1 = (bf16[28,896]{1,0:T(8,128)(2,1)S(1)}, bf16[28,896]{1,0:T(8,128)(2,1)S(1)}, u32[]{:S(2)}, u32[]{:S(2)}) collective-permute-start(bf16[28,896]{1,0:T(8,128)(2,1)S(1)} %multiply_convert_fusion.2), channel_id=1, source_target_pairs={{0,8},{1,32},{2,10},{3,34},{4,12},{5,36},{6,14},{7,38},{8,9},{9,33... | collective-permute-start | bytes 150536 | tf_op jit(solution)/shard_map/ppermute | solution.py:96
  176.8 0.7 reshape.61
  177.5 4.0 %collective-permute-done.1 = bf16[28,896]{1,0:T(8,128)(2,1)S(1)} collective-permute-done((bf16[28,896]{1,0:T(8,128)(2,1)S(1)}, bf16[28,896]{1,0:T(8,128)(2,1)S(1)}, u32[]{:S(2)}, u32[]{:S(2)}) %collective-permute-start.1) | collective-permute-done | bytes 50208 | tf_op jit(solution)/shard_map/ppermute | solution.py:96
  181.5 0.7 reshape.59
  (13 shorter events, 0.7 us)
Async XLA Ops:
  0.6 1.4 copy-start
  11.1 31.9 %all-to-all-start.3 = ((bf16[8,32,1792]{2,1,0:T(8,128)(2,1)}), bf16[8,32,1792]{2,1,0:T(8,128)(2,1)S(1)}, u32[]{:S(2)}, u32[]{:S(2)}) async-start(bf16[8,32,1792]{2,1,0:T(8,128)(2,1)} %fusion.35), calls=%async_computation.3 | async-start | bytes 1835008 | tf_op jit(solution)/shard_map/all_to_all | solution.py:66
  43.1 38.5 %all-to-all-start = ((bf16[8,32,1792]{2,1,0:T(8,128)(2,1)}), bf16[8,32,1792]{2,1,0:T(8,128)(2,1)S(1)}, u32[]{:S(2)}, u32[]{:S(2)}) async-start(bf16[8,32,1792]{2,1,0:T(8,128)(2,1)} %fusion.31), calls=%async_computation | async-start | bytes 1835008 | tf_op jit(solution)/shard_map/all_to_all | solution.py:66
  55.2 29.5 %collective-permute-start.2 = (bf16[256,1792]{1,0:T(8,128)(2,1)S(1)}, bf16[256,1792]{1,0:T(8,128)(2,1)S(1)}, u32[]{:S(2)}, u32[]{:S(2)}) collective-permute-start(bf16[256,1792]{1,0:T(8,128)(2,1)S(1)} %bitcast.72), channel_id=1, source_target_pairs={{0,1},{1,0},{2,3},{3,2},{4,5},{5,4},{6,7},{7,6},{8,9},{9,8},{10,11... | collective-permute-start | bytes 2752520 | tf_op jit(solution)/shard_map/ppermute | solution.py:70
  81.6 9.6 %collective-permute-start = (bf16[256,1792]{1,0:T(8,128)(2,1)S(1)}, bf16[256,1792]{1,0:T(8,128)(2,1)}, u32[]{:S(2)}, u32[]{:S(2)}) collective-permute-start(bf16[256,1792]{1,0:T(8,128)(2,1)S(1)} %bitcast.74), channel_id=1, source_target_pairs={{0,1},{1,0},{2,3},{3,2},{4,5},{5,4},{6,7},{7,6},{8,9},{9,8},{10,11... | collective-permute-start | bytes 2752520 | tf_op jit(solution)/shard_map/ppermute | solution.py:70
  86.5 24.9 %all-to-all-start.4 = ((bf16[4,224,896]{2,1,0:T(8,128)(2,1)}), bf16[4,224,896]{2,1,0:T(8,128)(2,1)S(1)}, u32[]{:S(2)}, u32[]{:S(2)}) async-start(bf16[4,224,896]{2,1,0:T(8,128)(2,1)} %bitcast.19), calls=%async_computation.4 | async-start | bytes 3211264 | tf_op jit(solution)/shard_map/all_to_all | solution.py:84
  111.4 23.5 %all-to-all-start.1 = ((bf16[4,224,896]{2,1,0:T(8,128)(2,1)}), bf16[4,224,896]{2,1,0:T(8,128)(2,1)S(1)}, u32[]{:S(2)}, u32[]{:S(2)}) async-start(bf16[4,224,896]{2,1,0:T(8,128)(2,1)} %bitcast.71), calls=%async_computation.1 | async-start | bytes 3211264 | tf_op jit(solution)/shard_map/all_to_all | solution.py:84
  134.9 17.6 %all-to-all-start.5 = ((bf16[8,28,896]{2,1,0:T(8,128)(2,1)}), bf16[8,28,896]{2,1,0:T(8,128)(2,1)S(1)}, u32[]{:S(2)}, u32[]{:S(2)}) async-start(bf16[8,28,896]{2,1,0:T(8,128)(2,1)} %reshape.57), calls=%async_computation.5 | async-start | bytes 917504 | tf_op jit(solution)/shard_map/all_to_all | solution.py:84
  152.5 16.4 %all-to-all-start.2 = ((bf16[8,28,896]{2,1,0:T(8,128)(2,1)}), bf16[8,28,896]{2,1,0:T(8,128)(2,1)S(1)}, u32[]{:S(2)}, u32[]{:S(2)}) async-start(bf16[8,28,896]{2,1,0:T(8,128)(2,1)} %reshape.54), calls=%async_computation.2 | async-start | bytes 917504 | tf_op jit(solution)/shard_map/all_to_all | solution.py:84
  156.1 20.7 %collective-permute-start.3 = (bf16[28,896]{1,0:T(8,128)(2,1)S(1)}, bf16[28,896]{1,0:T(8,128)(2,1)S(1)}, u32[]{:S(2)}, u32[]{:S(2)}) collective-permute-start(bf16[28,896]{1,0:T(8,128)(2,1)S(1)} %multiply_convert_fusion.1), channel_id=1, source_target_pairs={{0,8},{1,32},{2,10},{3,34},{4,12},{5,36},{6,14},{7,38},{8,56},{9,1... | collective-permute-start | bytes 150536 | tf_op jit(solution)/shard_map/ppermute | solution.py:97
  169.0 12.5 %collective-permute-start.1 = (bf16[28,896]{1,0:T(8,128)(2,1)S(1)}, bf16[28,896]{1,0:T(8,128)(2,1)S(1)}, u32[]{:S(2)}, u32[]{:S(2)}) collective-permute-start(bf16[28,896]{1,0:T(8,128)(2,1)S(1)} %multiply_convert_fusion.2), channel_id=1, source_target_pairs={{0,8},{1,32},{2,10},{3,34},{4,12},{5,36},{6,14},{7,38},{8,9},{9,33... | collective-permute-start | bytes 150536 | tf_op jit(solution)/shard_map/ppermute | solution.py:96

commit v3 on v2

v3 whole, which is shorter than its diff:
```python
import jax
import jax.numpy as jnp
import numpy as np
from jax import lax
from jax.experimental import pallas as pl
from jax.experimental.pallas import tpu as pltpu
from jax.sharding import Mesh
from jax.sharding import PartitionSpec as P

TOK = ("z", "yh", "x", "core")
ALL = ("task",) + TOK
YRING = ("yh", "task")
PAIRS = ((0, 1), (0, 2), (0, 3), (1, 2), (1, 3), (2, 3), (0, 1), (2, 3))
MIXED = 6
VMEM = pl.BlockSpec(memory_space=pltpu.VMEM)
SMEM = pl.BlockSpec(memory_space=pltpu.SMEM)


def tile_of(pair, second):
    i, j = PAIRS[pair]
    if pair < MIXED:
        return (j, i) if second else (i, j)
    return (j, j) if second else (i, i)


def routes(shape):
    n_task, n_z, n_yh, n_x, n_core = shape
    flat = np.arange(np.prod(shape)).reshape(shape)
    z_first, y_first = [], []
    for t, yh, x in np.ndindex(n_task, n_yh, n_x):
        z_first.append([int(d) for d in flat[t, :, yh, x, 0]])
        y_first.append([int(d) for d in flat[t, :, yh, x, 1]])
    for z, x in np.ndindex(n_z, n_x):
        for core, groups in ((1, z_first), (0, y_first)):
            groups.append([int(d) for yh in range(n_yh) for d in flat[:, z, yh, x, core]])
    homes = ([], [])
    for t, z, yh, x, core in np.ndindex(*shape):
        y = yh * n_task + t
        pair, rows = (z, y) if core == 0 else (y, z)
        for n in range(2):
            i, j = tile_of(pair, n != core)
            home = flat[x, 2 * i + j // 2, j % 2, rows // n_core, rows % n_core]
            homes[n].append((int(flat[t, z, yh, x, core]), int(home)))
    return z_first, y_first, homes


def normed(values, gain, live):
    scale = lax.rsqrt(jnp.mean(values * values, axis=-1, keepdims=True) + 1e-06)
    return (values * scale * gain * live).astype(jnp.bfloat16)


def norm_kernel(facts_ref, hidden_ref, extra_ref, gain_ref, keep_ref, send_ref):
    rows = hidden_ref.shape[0]
    live = (lax.broadcasted_iota(jnp.int32, (rows, 1), 0) < facts_ref[0]).astype(jnp.float32)
    first = hidden_ref[...].astype(jnp.float32)
    x_attn = normed(first, gain_ref[0:1, :], live)
    mixed = first + extra_ref[...].astype(jnp.float32)
    x_mlp = normed(mixed, gain_ref[1:2, :], live)

    @pl.when(facts_ref[1] == 0)
    def _():
        keep_ref[...] = x_attn
        send_ref[...] = x_mlp

    @pl.when(facts_ref[1] != 0)
    def _():
        keep_ref[...] = x_mlp
        send_ref[...] = x_attn


def norms(facts, hidden, extra, gains):
    block = jax.ShapeDtypeStruct(hidden.shape, jnp.bfloat16)
    return pl.pallas_call(
        norm_kernel,
        out_shape=(block, block),
        in_specs=[SMEM, VMEM, VMEM, VMEM],
        out_specs=(VMEM, VMEM),
    )(facts, hidden, extra, gains)


def deal_kernel(keep_ref, got_ref, out_ref):
    rows = keep_ref.shape[0]
    band = keep_ref.shape[1] // 4
    for p, pair in enumerate(PAIRS):
        for n, b in enumerate(pair):
            lanes = slice(n * band, (n + 1) * band)
            out_ref[p, :rows, lanes] = keep_ref[:, b * band : (b + 1) * band]
            out_ref[p, rows:, lanes] = got_ref[:, b * band : (b + 1) * band]


def dealt(keep, got):
    rows, width = keep.shape
    return pl.pallas_call(
        deal_kernel,
        out_shape=jax.ShapeDtypeStruct((len(PAIRS), 2 * rows, width // 2), jnp.bfloat16),
        in_specs=[VMEM, VMEM],
        out_specs=VMEM,
    )(keep, got)


def gram_kernel(facts_ref, seen_ref, out_ref):
    band = seen_ref.shape[1] // 2
    rows = band // len(PAIRS)
    for n in range(2):
        at = facts_ref[2] if n == 0 else 1 - facts_ref[2]
        right = seen_ref[:, pl.ds(pl.multiple_of(at * band, 128), band)]
        full = lax.dot_general(
            seen_ref[:, n * band : (n + 1) * band],
            right,
            (((0,), (0,)), ((), ())),
            preferred_element_type=jnp.float32,
        )
        for k in range(len(PAIRS)):
            part = full[k * rows : (k + 1) * rows].astype(jnp.bfloat16)
            out_ref[k, n * rows : (n + 1) * rows, :] = part


def grams(facts, seen):
    band = seen.shape[1] // 2
    return pl.pallas_call(
        gram_kernel,
        out_shape=jax.ShapeDtypeStruct((len(PAIRS), 2 * band // len(PAIRS), band), jnp.bfloat16),
        in_specs=[SMEM, VMEM],
        out_specs=VMEM,
    )(facts, seen)


def solution(mesh):
    shape = (mesh.shape["task"], 8, 2, 4, 2)
    grid = Mesh(mesh.devices.reshape(shape), ALL)
    z_first, y_first, homes = routes(shape)

    def per_device(hidden, attn_out, gain_attn, gain_mlp, lengths):
        rows = hidden.shape[1]
        band = hidden.shape[2] // 4
        n_x = lax.axis_size("x")
        tokens = rows * lax.axis_size(TOK)
        seq_len = tokens // lengths.shape[1]
        core = lax.axis_index("core")
        z = lax.axis_index("z")
        yh = lax.axis_index("yh")

        start = lax.axis_index(TOK) * rows
        which = start // seq_len
        limit = lax.dynamic_index_in_dim(lengths[0], which, keepdims=False)
        pair = jnp.where(core == 0, z, lax.axis_index(YRING))
        facts = jnp.stack(
            [limit - (start - which * seq_len), core, (pair < MIXED).astype(jnp.int32)]
        )
        gains = jnp.stack([gain_attn, gain_mlp]).astype(jnp.float32)

        def swapped(part, groups):
            return lax.all_to_all(
                part, ALL, split_axis=0, concat_axis=0, axis_index_groups=groups, tiled=True
            )

        keep, send = norms(facts, hidden[0], attn_out[0], gains)
        got = lax.ppermute(send, "core", [(0, 1), (1, 0)])
        seen = swapped(dealt(keep, got), z_first).reshape(-1, 2 * band)
        part = swapped(grams(facts, seen), y_first)
        half = part.astype(jnp.float32).sum(axis=0).reshape(2, n_x, -1, band)
        half = half.transpose(1, 0, 2, 3).reshape(n_x, -1, band).astype(jnp.bfloat16)
        last = lax.all_to_all(half, "x", split_axis=0, concat_axis=0, tiled=True)
        last = last.astype(jnp.float32).sum(axis=0).reshape(2, -1, band) * (1.0 / tokens)
        last = last.astype(jnp.bfloat16)
        same = lax.ppermute(jnp.where(core == 0, last[0], last[1]), ALL, homes[0])
        other = lax.ppermute(jnp.where(core == 0, last[1], last[0]), ALL, homes[1])
        i, j = z // 2, z % 2 * 2 + yh
        upper = (i < j) | ((i == j) & (i % 2 == 0))
        out_attn = jnp.where(upper, same, other).astype(jnp.float32)
        out_mlp = jnp.where(upper, other, same).astype(jnp.float32)
        return out_attn[None], out_mlp[None]

    return jax.shard_map(
        per_device,
        mesh=grid,
        in_specs=(P("task", TOK, None), P("task", TOK, None), P(), P(), P("task", None)),
        out_specs=(P(TOK, "task", None), P(TOK, "task", None)),
        check_vma=False,
    )
```

time: 183 us -> 141 us (0.77)
  waiting for transfers between devices: 102 us -> 11.3 us
  blocking collectives: 0 us -> 88.8 us
  starting transfers between devices: 51.5 us -> 19.4 us
  Pallas kernels: 0 us -> 9.88 us
  other arithmetic: 10.2 us -> 2.68 us
  matrix products: 6.22 us -> 0 us
  local copies, waits for them, and re-layouts: 11.2 us -> 5.46 us
    all_to_all x6 -> x0, waiting for transfers between devices: 98.3 us -> none  [the longest x4 55.5 us: reduced(): got = lax.all_to_all(part, ring, split_axis=0, concat_axis=0, tiled=True)]
    all_to_all x0 -> x3, blocking collectives: none -> 88.8 us  [the longest x2 78.7 us: swapped(): lax.all_to_all(part, ALL, split_axis=0, concat_axis=0, axis_index_groups=...]
    all_to_all x6 -> x0, starting transfers between devices: 34.3 us -> none  [the longest x2 19.8 us: spread(): return lax.all_to_all(out, ring, split_axis=0, concat_axis=0, tiled=True)]
    pallas_call x0 -> x3, Pallas kernels: none -> 9.88 us  [the longest x1 5.29 us: grams(): pl.pallas_call(gram_kernel, out_shape=jax.ShapeDtypeStruct((len(PAIRS), 2...]
    ppermute x4 -> x3, waiting for transfers between devices: 3.97 us -> 11.3 us  [the longest x1 10 us: per_device(): same = lax.ppermute(jnp.where(core == 0, last[0], last[1]), ALL, homes[0])]
    dot_general x4 -> x0, matrix products: 6.22 us -> none  [product(): lax.dot_general(left, right, (((0,), (0,)), ((), ())), preferred_element_...]
    unnamed x10 -> x4, local copies, waits for them, and re-layouts: 5.19 us -> 0.71 us
    unnamed x6 -> x0, other arithmetic: 3.94 us -> none
  transfers between devices with their start and end apart: 10 -> 3, of which waited for: 7 -> 2; matrix products, arithmetic and copies ran while one was open for 9% -> 0% of each run, Pallas kernels for 0% -> 0%
where the time goes in v3:
time: 141 us; the launch traced here: 139 us
  blocking collectives  88.8 us (63%)
  starting transfers between devices  19.4 us (14%)
  waiting for transfers between devices  11.3 us (8%)
  Pallas kernels  9.88 us (7%)
  local copies, waits for them, and re-layouts  5.46 us (4%)
  other arithmetic  2.68 us (2%)
  between operations  1.47 us (1%)
    all_to_all x2, blocking collectives, swapped(): lax.all_to_all(part, ALL, split_axis=0, concat_axis=0, axis_index_groups=...  78.7 us
    all_to_all x1, blocking collectives, per_device(): last = lax.all_to_all(half, 'x', split_axis=0, concat_axis=0, tiled=True)  10.1 us
    ppermute x1, waiting for transfers between devices, per_device(): same = lax.ppermute(jnp.where(core == 0, last[0], last[1]), ALL, homes[0])  10 us
    ppermute x1, starting transfers between devices, per_device(): got = lax.ppermute(send, 'core', [(0, 1), (1, 0)])  8.74 us
    ppermute x1, starting transfers between devices, per_device(): other = lax.ppermute(jnp.where(core == 0, last[1], last[0]), ALL, homes[1])  6.74 us
    pallas_call x1, Pallas kernels, grams(): pl.pallas_call(gram_kernel, out_shape=jax.ShapeDtypeStruct((len(PAIRS), 2...  5.29 us
    ppermute x1, starting transfers between devices, per_device(): same = lax.ppermute(jnp.where(core == 0, last[0], last[1]), ALL, homes[0])  3.91 us
  transfers between devices with their start and end apart: 3, of which 2 were waited for; matrix products, arithmetic and copies ran while one was open for 0% of the time, Pallas kernels for 0%

profile of v3, /device:TPU:1, one launch (start us, length us, event | category | flops | bytes accessed | tf_op | source)
XLA Modules:
  0.0 139.0 jit_solution(7248052339342248004)
XLA Ops:
  0.6 0.0 copy-start
  0.7 0.7 stack.29
  1.4 0.7 stack.30
  2.1 0.0 copy-done
  2.1 0.6 constant_dynamic-slice_fusion
  3.4 0.6 maximum_convert_fusion.gain_ref
  4.0 0.6 pad_add_fusion.facts_ref
  4.6 2.2 %shard_map.68 = (bf16[32,3584]{1,0:T(8,128)(2,1)}, bf16[32,3584]{1,0:T(8,128)(2,1)}) custom-call(s32[3]{0:T(128)} %pad_add_fusion.facts_ref, bf16[32,3584]{1,0:T(8,128)(2,1)} %bitcast.12, bf16[32,3584]{1,0:T(8,128)(2,1)} %bitcast.13, f32[2,3584]{1,0:T(2,128)} %maximum_convert_fusion.gain_ref), custom_call_target="tpu_custom_call" | custom-call | tf_op jit(solution)/shard_map/pallas_call | solution.py:73
  6.8 8.7 %collective-permute-start = (bf16[32,3584]{1,0:T(8,128)(2,1)}, bf16[32,3584]{1,0:T(8,128)(2,1)S(1)}, u32[]{:S(2)}, u32[]{:S(2)}) collective-permute-start(bf16[32,3584]{1,0:T(8,128)(2,1)} %get-tuple-element.5), channel_id=1, source_target_pairs={{0,1},{1,0},{2,3},{3,2},{4,5},{5,4},{6,7},{7,6},{8,9},{9,8},{10,11... | collective-permute-start | bytes 688136 | tf_op jit(solution)/shard_map/ppermute | solution.py:158
  15.5 1.3 collective-permute-done.got_ref
  16.8 0.0 copy-start.1
  16.8 0.7 copy-done.1
  17.5 2.4 %shard_map.69 = bf16[8,64,1792]{2,1,0:T(8,128)(2,1)} custom-call(bf16[32,3584]{1,0:T(8,128)(2,1)} %get-tuple-element.4.keep_ref, bf16[32,3584]{1,0:T(8,128)(2,1)} %copy-done.1), custom_call_target="tpu_custom_call" | custom-call | tf_op jit(solution)/shard_map/pallas_call | solution.py:93
  20.0 30.5 %all_to_all.15 = bf16[8,64,1792]{2,1,0:T(8,128)(2,1)} all-to-all(bf16[8,64,1792]{2,1,0:T(8,128)(2,1)} %shard_map.69), channel_id=1, replica_groups={{0,16,32,48,64,80,96,112},{2,18,34,50,66,82,98,114},{4,20,36,52,68,84,1..., dimensions={0} | all-to-all | bytes 3670016 | tf_op jit(solution)/shard_map/all_to_all | solution.py:153
  50.4 5.3 %shard_map.70 = bf16[8,224,896]{2,1,0:T(8,128)(2,1)} custom-call(s32[3]{0:T(128)} %pad_add_fusion.facts_ref, bf16[512,1792]{1,0:T(8,128)(2,1)} %bitcast.9), custom_call_target="tpu_custom_call" | custom-call | tf_op jit(solution)/shard_map/pallas_call | solution.py:120
  55.7 48.2 %all_to_all.16 = bf16[8,224,896]{2,1,0:T(8,128)(2,1)S(1)} all-to-all(bf16[8,224,896]{2,1,0:T(8,128)(2,1)} %shard_map.70), channel_id=1, replica_groups={{1,17,33,49,65,81,97,113},{3,19,35,51,67,83,99,115},{5,21,37,53,69,85,1..., dimensions={0} | all-to-all | bytes 6422528 | tf_op jit(solution)/shard_map/all_to_all | solution.py:153
  104.0 1.3 reduce_sum.21
  105.3 1.1 convert_element_type.25
  106.3 0.2 copy.8
  106.6 10.1 %all_to_all.17 = bf16[4,56,896]{2,1,0:T(8,128)(2,1)S(1)} all-to-all(bf16[4,56,896]{2,1,0:T(8,128)(2,1)S(1)} %copy.9), channel_id=1, replica_groups=mesh['task'=4,'z'=8,'yh'=2,'x'=4,'core'=2] {'x'}, dimensions={0} | all-to-all | bytes 802816 | tf_op jit(solution)/shard_map/all_to_all | solution.py:163
  116.7 0.1 convert_reduce_fusion
  116.8 6.7 %collective-permute-start.2 = (bf16[28,896]{1,0:T(8,128)(2,1)S(1)}, bf16[28,896]{1,0:T(8,128)(2,1)S(1)}, u32[]{:S(2)}, u32[]{:S(2)}) collective-permute-start(bf16[28,896]{1,0:T(8,128)(2,1)S(1)} %get-tuple-element.8), channel_id=1, source_target_pairs={{0,32},{1,8},{2,160},{3,136},{4,288},{5,264},{6,416},{7,392},{8,36... | collective-permute-start | bytes 150536 | tf_op jit(solution)/shard_map/ppermute | solution.py:167
  123.6 3.9 %collective-permute-start.1 = (bf16[28,896]{1,0:T(8,128)(2,1)S(1)}, bf16[28,896]{1,0:T(8,128)(2,1)S(1)}, u32[]{:S(2)}, u32[]{:S(2)}) collective-permute-start(bf16[28,896]{1,0:T(8,128)(2,1)S(1)} %get-tuple-element.9), channel_id=1, source_target_pairs={{0,8},{1,32},{2,136},{3,160},{4,264},{5,288},{6,392},{7,416},{8,12... | collective-permute-start | bytes 150536 | tf_op jit(solution)/shard_map/ppermute | solution.py:166
  127.5 0.0 collective-permute-done.2
  127.6 10.0 %collective-permute-done.1 = bf16[28,896]{1,0:T(8,128)(2,1)S(1)} collective-permute-done((bf16[28,896]{1,0:T(8,128)(2,1)S(1)}, bf16[28,896]{1,0:T(8,128)(2,1)S(1)}, u32[]{:S(2)}, u32[]{:S(2)}) %collective-permute-start.1) | collective-permute-done | bytes 50208 | tf_op jit(solution)/shard_map/ppermute | solution.py:166
  137.6 0.7 reshape.32
  138.3 0.7 reshape.31
  (4 shorter events, 0.1 us)
Async XLA Ops:
  0.6 1.5 %copy-start = (s32[1,2]{1,0:T(1,128)S(1)}, s32[1,2]{1,0:T(1,128)}, u32[]{:S(2)}) copy-start(s32[1,2]{1,0:T(1,128)} %param.9) | copy-start | bytes 28
  6.8 10.0 %collective-permute-start = (bf16[32,3584]{1,0:T(8,128)(2,1)}, bf16[32,3584]{1,0:T(8,128)(2,1)S(1)}, u32[]{:S(2)}, u32[]{:S(2)}) collective-permute-start(bf16[32,3584]{1,0:T(8,128)(2,1)} %get-tuple-element.5), channel_id=1, source_target_pairs={{0,1},{1,0},{2,3},{3,2},{4,5},{5,4},{6,7},{7,6},{8,9},{9,8},{10,11... | collective-permute-start | bytes 688136 | tf_op jit(solution)/shard_map/ppermute | solution.py:158
  16.8 0.7 copy-start.1
  116.8 10.7 %collective-permute-start.2 = (bf16[28,896]{1,0:T(8,128)(2,1)S(1)}, bf16[28,896]{1,0:T(8,128)(2,1)S(1)}, u32[]{:S(2)}, u32[]{:S(2)}) collective-permute-start(bf16[28,896]{1,0:T(8,128)(2,1)S(1)} %get-tuple-element.8), channel_id=1, source_target_pairs={{0,32},{1,8},{2,160},{3,136},{4,288},{5,264},{6,416},{7,392},{8,36... | collective-permute-start | bytes 150536 | tf_op jit(solution)/shard_map/ppermute | solution.py:167
  123.6 14.0 %collective-permute-start.1 = (bf16[28,896]{1,0:T(8,128)(2,1)S(1)}, bf16[28,896]{1,0:T(8,128)(2,1)S(1)}, u32[]{:S(2)}, u32[]{:S(2)}) collective-permute-start(bf16[28,896]{1,0:T(8,128)(2,1)S(1)} %get-tuple-element.9), channel_id=1, source_target_pairs={{0,8},{1,32},{2,136},{3,160},{4,264},{5,288},{6,392},{7,416},{8,12... | collective-permute-start | bytes 150536 | tf_op jit(solution)/shard_map/ppermute | solution.py:166

commit v4 on v3

v4 whole, which is shorter than its diff:
```python
import jax
import jax.numpy as jnp
import numpy as np
from jax import lax
from jax.experimental import pallas as pl
from jax.experimental.pallas import tpu as pltpu
from jax.sharding import Mesh
from jax.sharding import PartitionSpec as P

TOK = ("z", "yh", "x", "core")
ALL = ("task",) + TOK
YRING = ("yh", "task")
PAIRS = ((0, 1), (0, 2), (0, 3), (1, 2), (1, 3), (2, 3), (0, 1), (2, 3))
MIXED = 6
VMEM = pl.BlockSpec(memory_space=pltpu.VMEM)
SMEM = pl.BlockSpec(memory_space=pltpu.SMEM)


def tile_of(pair, second):
    i, j = PAIRS[pair]
    if pair < MIXED:
        return (j, i) if second else (i, j)
    return (j, j) if second else (i, i)


def layout(shape, rows, seq_len):
    n_task, n_z, n_yh, n_x, n_core = shape
    n_y = n_yh * n_task
    flat = np.arange(np.prod(shape)).reshape(shape)
    gather, cube, line = {}, {}, {}
    home = []
    facts = np.zeros((flat.size, 4), np.int32)
    for t, z, yh, x, core in np.ndindex(*shape):
        me = int(flat[t, z, yh, x, core])
        y = yh * n_task + t
        a, m, n = (x, z, y) if core == 0 else ((x + 1) % n_x, (y + 1) % n_y, (z + 1) % n_z)
        pair = m // 2 * 2 + a // 2
        corner = a % 2 * 4 + m % 2 * 2 + n % 2
        step = n // 2
        gather.setdefault((core, a % 2, m % 2, n), {})[pair] = me
        cube.setdefault((core, m // 2, a // 2, n // 2), {})[corner] = me
        line.setdefault((core, a, m, n % 2), {})[step] = me
        i, j = tile_of(pair, corner // 2 % 2)
        to_x = step // 2 * 2 + corner // 4
        to_t = step % 2 * 2 + corner % 2
        home.append((me, int(flat[to_t, 2 * i + j // 2, j % 2, to_x, core])))
        first = (((z * n_yh + yh) * n_x + x) * n_core + core) * rows
        facts[me] = (core, pair < MIXED, first // seq_len, first % seq_len)

    def listed(groups):
        return [[group[k] for k in sorted(group)] for group in groups.values()]

    return listed(gather), listed(cube), listed(line), home, facts


def normed(values, gain, live):
    scale = lax.rsqrt(jnp.mean(values * values, axis=-1, keepdims=True) + 1e-06)
    return (values * scale * gain * live).astype(jnp.bfloat16)


def norm_kernel(facts_ref, lengths_ref, hidden_ref, extra_ref, gain_ref, keep_ref, send_ref):
    rows = hidden_ref.shape[0]
    place = lax.broadcasted_iota(jnp.int32, (rows, 1), 0) + facts_ref[3]
    live = (place < lengths_ref[0, facts_ref[2]]).astype(jnp.float32)
    first = hidden_ref[...].astype(jnp.float32)
    x_attn = normed(first, gain_ref[0:1, :], live)
    mixed = first + extra_ref[...].astype(jnp.float32)
    x_mlp = normed(mixed, gain_ref[1:2, :], live)

    @pl.when(facts_ref[0] == 0)
    def _():
        keep_ref[...] = x_attn
        send_ref[...] = x_mlp

    @pl.when(facts_ref[0] != 0)
    def _():
        keep_ref[...] = x_mlp
        send_ref[...] = x_attn


def norms(facts, lengths, hidden, extra, gains):
    block = jax.ShapeDtypeStruct(hidden.shape, jnp.bfloat16)
    return pl.pallas_call(
        norm_kernel,
        out_shape=(block, block),
        in_specs=[SMEM, SMEM, VMEM, VMEM, VMEM],
        out_specs=(VMEM, VMEM),
    )(facts, lengths, hidden, extra, gains)


def deal_kernel(keep_ref, got_ref, out_ref):
    rows = keep_ref.shape[0]
    band = keep_ref.shape[1] // 4
    for p, pair in enumerate(PAIRS):
        for n, b in enumerate(pair):
            lanes = slice(n * band, (n + 1) * band)
            out_ref[p, :rows, lanes] = keep_ref[:, b * band : (b + 1) * band]
            out_ref[p, rows:, lanes] = got_ref[:, b * band : (b + 1) * band]


def dealt(keep, got):
    rows, width = keep.shape
    return pl.pallas_call(
        deal_kernel,
        out_shape=jax.ShapeDtypeStruct((len(PAIRS), 2 * rows, width // 2), jnp.bfloat16),
        in_specs=[VMEM, VMEM],
        out_specs=VMEM,
    )(keep, got)


def gram_kernel(facts_ref, seen_ref, out_ref):
    band = seen_ref.shape[1] // 2
    rows = band // len(PAIRS)
    for n in range(2):
        at = facts_ref[1] if n == 0 else 1 - facts_ref[1]
        right = seen_ref[:, pl.ds(pl.multiple_of(at * band, 128), band)]
        full = lax.dot_general(
            seen_ref[:, n * band : (n + 1) * band],
            right,
            (((0,), (0,)), ((), ())),
            preferred_element_type=jnp.float32,
        )
        for low_x, low_t in np.ndindex(2, 2):
            pieces = []
            for high_x, high_t, low in np.ndindex(2, 2, 2):
                at = (high_x * 4 + low_x * 2 + low) * rows + (high_t * 2 + low_t) * (rows // 4)
                pieces.append(full[at : at + rows // 4])
            chunk = jnp.concatenate(pieces, axis=0).astype(jnp.bfloat16)
            out_ref[low_x * 4 + n * 2 + low_t] = chunk


def grams(facts, seen):
    band = seen.shape[1] // 2
    return pl.pallas_call(
        gram_kernel,
        out_shape=jax.ShapeDtypeStruct((len(PAIRS), 2 * band // len(PAIRS), band), jnp.bfloat16),
        in_specs=[SMEM, VMEM],
        out_specs=VMEM,
    )(facts, seen)


def solution(mesh):
    shape = (mesh.shape["task"], 8, 2, 4, 2)
    grid = Mesh(mesh.devices.reshape(shape), ALL)

    def per_device(hidden, attn_out, gain_attn, gain_mlp, lengths):
        rows = hidden.shape[1]
        band = hidden.shape[2] // 4
        piece = band // 32
        tokens = rows * lax.axis_size(TOK)
        gather, cube, line, home, table = layout(shape, rows, tokens // lengths.shape[1])
        core = lax.axis_index("core")
        facts = lax.dynamic_index_in_dim(jnp.asarray(table), lax.axis_index(ALL), 0, False)
        gains = jnp.stack([gain_attn, gain_mlp]).astype(jnp.float32)

        def swapped(part, groups):
            return lax.all_to_all(
                part, ALL, split_axis=0, concat_axis=0, axis_index_groups=groups, tiled=True
            )

        def core_swap(part):
            return lax.ppermute(part, "core", [(0, 1), (1, 0)])

        keep, send = norms(facts, lengths, hidden[0], attn_out[0], gains)
        seen = swapped(dealt(keep, core_swap(send)), gather).reshape(-1, 2 * band)
        part = swapped(grams(facts, seen), cube)
        half = part.astype(jnp.float32).sum(axis=0).astype(jnp.bfloat16)
        last = swapped(half.reshape(4, 2 * piece, band), line)
        last = last.astype(jnp.float32).sum(axis=0) * (1.0 / tokens)
        mine = lax.ppermute(last.astype(jnp.bfloat16), ALL, home)
        own = jnp.where(core == 0, mine[:piece], mine[piece:])
        got = core_swap(jnp.where(core == 0, mine[piece:], mine[:piece]))
        out_attn = jnp.where(core == 0, own, got).astype(jnp.float32)
        out_mlp = jnp.where(core == 0, got, own).astype(jnp.float32)
        return out_attn[None], out_mlp[None]

    return jax.shard_map(
        per_device,
        mesh=grid,
        in_specs=(P("task", TOK, None), P("task", TOK, None), P(), P(), P("task", None)),
        out_specs=(P(TOK, "task", None), P(TOK, "task", None)),
        check_vma=False,
    )
```

time: 141 us -> 126 us (0.89)
  the two profiles are of different devices: /device:TPU:1 before, /device:TPU:13 now
where the time goes in v4:
time: 126 us; the launch traced here: 125 us
  blocking collectives  78.6 us (62%)
  starting transfers between devices  15 us (12%)
  waiting for transfers between devices  14 us (11%)
  Pallas kernels  9.91 us (8%)
  local copies, waits for them, and re-layouts  4.84 us (4%)
  other arithmetic  2.05 us (2%)
    all_to_all x3, blocking collectives, swapped(): lax.all_to_all(part, ALL, split_axis=0, concat_axis=0, axis_index_groups=...  78.6 us
    ppermute x1, waiting for transfers between devices, per_device(): mine = lax.ppermute(last.astype(jnp.bfloat16), ALL, home)  11.8 us
    ppermute x2, starting transfers between devices, core_swap(): return lax.ppermute(part, 'core', [(0, 1), (1, 0)])  11.7 us
    pallas_call x1, Pallas kernels, grams(): pl.pallas_call(gram_kernel, out_shape=jax.ShapeDtypeStruct((len(PAIRS), 2...  5.28 us
    ppermute x1, starting transfers between devices, per_device(): mine = lax.ppermute(last.astype(jnp.bfloat16), ALL, home)  3.28 us
  transfers between devices with their start and end apart: 3, of which 3 were waited for; matrix products, arithmetic and copies ran while one was open for 0% of the time, Pallas kernels for 0%

profile of v4, /device:TPU:13, one launch (start us, length us, event | category | flops | bytes accessed | tf_op | source)
XLA Modules:
  0.0 125.0 jit_solution(15682186251445002638)
XLA Ops:
  0.6 0.7 stack.9
  1.4 0.7 stack.10
  2.1 1.2 dynamic-slice_bitcast_fusion.facts_ref
  3.3 0.6 maximum_convert_fusion.gain_ref
  3.9 2.2 %shard_map.77 = (bf16[32,3584]{1,0:T(8,128)(2,1)}, bf16[32,3584]{1,0:T(8,128)(2,1)}) custom-call(s32[4]{0:T(128)} %dynamic-slice_bitcast_fusion.facts_ref, s32[1,2]{1,0:T(1,128)} %lengths_ref.1, bf16[32,3584]{1,0:T(8,128)(2,1)} %bitcast.14, bf16[32,3584]{1,0:T(8,128)(2,1)} %bitcast.15, f32[2,3584]{1,0:T(2,128)} %maximum_convert_fusion.gain_ref), custom_call_target="tpu_custom_call" | custom-call | tf_op jit(solution)/shard_map/pallas_call | solution.py:83
  6.1 2.6 %collective-permute-start = (bf16[32,3584]{1,0:T(8,128)(2,1)}, bf16[32,3584]{1,0:T(8,128)(2,1)S(1)}, u32[]{:S(2)}, u32[]{:S(2)}) collective-permute-start(bf16[32,3584]{1,0:T(8,128)(2,1)} %get-tuple-element.5), channel_id=1, source_target_pairs={{0,1},{1,0},{2,3},{3,2},{4,5},{5,4},{6,7},{7,6},{8,9},{9,8},{10,11... | collective-permute-start | bytes 688136 | tf_op jit(solution)/shard_map/ppermute | solution.py:162
  8.7 1.3 %collective-permute-done.got_ref = bf16[32,3584]{1,0:T(8,128)(2,1)S(1)} collective-permute-done((bf16[32,3584]{1,0:T(8,128)(2,1)}, bf16[32,3584]{1,0:T(8,128)(2,1)S(1)}, u32[]{:S(2)}, u32[]{:S(2)}) %collective-permute-start) | collective-permute-done | bytes 229408 | tf_op jit(solution)/shard_map/ppermute | solution.py:162
  10.0 0.0 copy-start
  10.0 0.7 copy-done
  10.7 2.4 %shard_map.78 = bf16[8,64,1792]{2,1,0:T(8,128)(2,1)} custom-call(bf16[32,3584]{1,0:T(8,128)(2,1)} %get-tuple-element.4.keep_ref, bf16[32,3584]{1,0:T(8,128)(2,1)} %copy-done), custom_call_target="tpu_custom_call" | custom-call | tf_op jit(solution)/shard_map/pallas_call | solution.py:103
  13.2 32.4 %all_to_all.15 = bf16[8,64,1792]{2,1,0:T(8,128)(2,1)} all-to-all(bf16[8,64,1792]{2,1,0:T(8,128)(2,1)} %shard_map.78), channel_id=1, replica_groups={{0,4,32,36,64,68,96,100},{1,5,257,261,9,13,265,269},{2,6,34,38,66,70,98..., dimensions={0} | all-to-all | bytes 3670016 | tf_op jit(solution)/shard_map/all_to_all | solution.py:157
  45.5 5.3 %shard_map.79 = bf16[8,224,896]{2,1,0:T(8,128)(2,1)} custom-call(s32[4]{0:T(128)} %dynamic-slice_bitcast_fusion.facts_ref, bf16[512,1792]{1,0:T(8,128)(2,1)} %bitcast.12), custom_call_target="tpu_custom_call" | custom-call | tf_op jit(solution)/shard_map/pallas_call | solution.py:134
  50.8 31.9 %all_to_all.16 = bf16[8,224,896]{2,1,0:T(8,128)(2,1)S(1)} all-to-all(bf16[8,224,896]{2,1,0:T(8,128)(2,1)} %shard_map.79), channel_id=1, replica_groups={{0,128,16,144,2,130,18,146},{511,399,119,7,505,393,113,1},{507,395,115,..., dimensions={0} | all-to-all | bytes 6422528 | tf_op jit(solution)/shard_map/all_to_all | solution.py:157
  82.8 1.3 %reduce_sum.21 = bf16[224,896]{1,0:T(8,128)(2,1)} reduce(bf16[8,224,896]{2,1,0:T(8,128)(2,1)S(1)} %all_to_all.16, bf16[]{:T(256)} %constant.39.clone.1), dimensions={0}, to_apply=%region_0.1 | reduce | flops 1404928 | bytes 3612674 | tf_op jit(solution)/shard_map/reduce_sum | solution.py:167
  84.0 14.2 %all_to_all.17 = bf16[4,56,896]{2,1,0:T(8,128)(2,1)S(1)} all-to-all(bf16[4,56,896]{2,1,0:T(8,128)(2,1)} %bitcast.13), channel_id=1, replica_groups={{0,256,8,264},{1,33,65,97},{2,258,10,266},{3,35,67,99},{4,260,12,268},{..., dimensions={0} | all-to-all | bytes 802816 | tf_op jit(solution)/shard_map/all_to_all | solution.py:157
  98.3 0.1 convert_reduce_fusion
  98.3 3.3 %collective-permute-start.1 = (bf16[56,896]{1,0:T(8,128)(2,1)S(1)}, bf16[56,896]{1,0:T(8,128)(2,1)S(1)}, u32[]{:S(2)}, u32[]{:S(2)}) collective-permute-start(bf16[56,896]{1,0:T(8,128)(2,1)S(1)} %multiply_convert_fusion), channel_id=1, source_target_pairs={{0,8},{1,163},{2,10},{3,193},{4,16},{5,195},{6,18},{7,161},{8,12},... | collective-permute-start | bytes 301064 | tf_op jit(solution)/shard_map/ppermute | solution.py:170
  101.6 11.8 %collective-permute-done.1 = bf16[56,896]{1,0:T(8,128)(2,1)S(1)} collective-permute-done((bf16[56,896]{1,0:T(8,128)(2,1)S(1)}, bf16[56,896]{1,0:T(8,128)(2,1)S(1)}, u32[]{:S(2)}, u32[]{:S(2)}) %collective-permute-start.1) | collective-permute-done | bytes 100384 | tf_op jit(solution)/shard_map/ppermute | solution.py:170
  113.5 9.1 %collective-permute-start.2 = (bf16[28,896]{1,0:T(8,128)(2,1)S(1)}, bf16[28,896]{1,0:T(8,128)(2,1)S(1)}, u32[]{:S(2)}, u32[]{:S(2)}) collective-permute-start(bf16[28,896]{1,0:T(8,128)(2,1)S(1)} %broadcast_select_fusion), channel_id=1, source_target_pairs={{0,1},{1,0},{2,3},{3,2},{4,5},{5,4},{6,7},{7,6},{8,9},{9,8},{10,11... | collective-permute-start | bytes 150536 | tf_op jit(solution)/shard_map/ppermute | solution.py:162
  122.6 0.9 collective-permute-done.2
  123.5 0.7 copy.9
  124.2 0.7 copy.8
  (3 shorter events, 0.1 us)
Async XLA Ops:
  6.1 3.9 %collective-permute-start = (bf16[32,3584]{1,0:T(8,128)(2,1)}, bf16[32,3584]{1,0:T(8,128)(2,1)S(1)}, u32[]{:S(2)}, u32[]{:S(2)}) collective-permute-start(bf16[32,3584]{1,0:T(8,128)(2,1)} %get-tuple-element.5), channel_id=1, source_target_pairs={{0,1},{1,0},{2,3},{3,2},{4,5},{5,4},{6,7},{7,6},{8,9},{9,8},{10,11... | collective-permute-start | bytes 688136 | tf_op jit(solution)/shard_map/ppermute | solution.py:162
  10.0 0.7 copy-start
  98.3 15.1 %collective-permute-start.1 = (bf16[56,896]{1,0:T(8,128)(2,1)S(1)}, bf16[56,896]{1,0:T(8,128)(2,1)S(1)}, u32[]{:S(2)}, u32[]{:S(2)}) collective-permute-start(bf16[56,896]{1,0:T(8,128)(2,1)S(1)} %multiply_convert_fusion), channel_id=1, source_target_pairs={{0,8},{1,163},{2,10},{3,193},{4,16},{5,195},{6,18},{7,161},{8,12},... | collective-permute-start | bytes 301064 | tf_op jit(solution)/shard_map/ppermute | solution.py:170
  113.5 10.0 %collective-permute-start.2 = (bf16[28,896]{1,0:T(8,128)(2,1)S(1)}, bf16[28,896]{1,0:T(8,128)(2,1)S(1)}, u32[]{:S(2)}, u32[]{:S(2)}) collective-permute-start(bf16[28,896]{1,0:T(8,128)(2,1)S(1)} %broadcast_select_fusion), channel_id=1, source_target_pairs={{0,1},{1,0},{2,3},{3,2},{4,5},{5,4},{6,7},{7,6},{8,9},{9,8},{10,11... | collective-permute-start | bytes 150536 | tf_op jit(solution)/shard_map/ppermute | solution.py:162
